TPU v7x, 32 devices: a whole 2x2x4 slice. The times are simulated.
32 devices in a mesh: rep: 32 (over z, y, x, core).
Axes of the slice: x: 2, y: 2, z: 4, core: 2. Of those that a mesh axis runs over, the one named last changes fastest.
Arguments:
- inputs: bfloat16 [16384, 1024], P('rep'), may hold values from -6 to 6
- out_grads: bfloat16 [16384, 4096], P('rep'), may hold values from -0.29882812 to 0.29882812
- error_in: bfloat16 [32, 1024, 4096], P('rep'), may hold values from -6 to 6
- q_start: float32 [32, 4096], replicated, may hold values from -0.09375 to 0.09375
- master: float32 [1024, 4096], P(None, 'rep'), may hold values from -1.2 to 1.2
Outputs:
- error_out: bfloat16 [32, 1024, 4096], P('rep')
- q_out: float32 [32, 4096], replicated
- master_out: float32 [1024, 4096], P(None, 'rep')
All inputs are finite; a program needn't handle non-finite values.
Results may differ from a plain program's by a relative error of at most 0.001.
Values sent between devices are 32-bit elements; how exact they have to be, the bound alone decides.
No kernel may reach another device: no remote copies, remote signals or barrier semaphores. Data moves between devices by JAX's collectives and lax.ppermute only.
A program may use at most 128 MiB of HBM per device.

v0:
```python
import jax
import jax.numpy as jnp
from jax import lax
from jax.sharding import PartitionSpec as P

ITERS = 3


def orthonormal(rows):
    basis = jnp.zeros_like(rows)
    for k in range(rows.shape[0]):
        vector = rows[k]
        coef = jnp.dot(basis, vector, precision=lax.Precision.HIGHEST)
        vector = vector - jnp.dot(coef, basis, precision=lax.Precision.HIGHEST)
        basis = basis.at[k].set(vector / jnp.sqrt(jnp.sum(vector * vector) + 1.0))
    return basis


def outer_rows(left, right):
    return lax.dot_general(
        left,
        right,
        (((0,), (0,)), ((), ())),
        precision=lax.Precision.HIGHEST,
        preferred_element_type=jnp.float32,
    )


def shards(inputs, out_grads, error_in, q_start, master):
    count = lax.axis_size("rep")
    grad = lax.dot_general(
        inputs, out_grads, (((0,), (0,)), ((), ())), preferred_element_type=jnp.float32
    )
    merged = grad + error_in[0].astype(jnp.float32)
    factor = q_start
    basis = None
    local_q = None
    for step in range(ITERS):
        local_p = lax.dot_general(
            factor,
            merged,
            (((1,), (1,)), ((), ())),
            precision=lax.Precision.HIGHEST,
            preferred_element_type=jnp.float32,
        )
        total_p = lax.psum(local_p, "rep")
        basis = orthonormal(total_p)
        local_q = jnp.dot(
            basis, merged, precision=lax.Precision.HIGHEST, preferred_element_type=jnp.float32
        )
        if step + 1 < ITERS:
            factor = lax.psum(local_q, "rep") / count
    width = master.shape[1]
    factor = lax.psum(local_q, "rep") / count
    recon = outer_rows(basis, factor)
    own_cols = lax.dynamic_slice_in_dim(recon, lax.axis_index("rep") * width, width, 1)
    master_out = master - 0.5 * own_cols
    error_out = (merged - recon).astype(jnp.bfloat16)[None]
    return (error_out, factor, master_out)


def solution(mesh):
    return jax.shard_map(
        shards,
        mesh=mesh,
        in_specs=(P("rep", None), P("rep", None), P("rep", None, None), P(), P(None, "rep")),
        out_specs=(P("rep", None, None), P(), P(None, "rep")),
        check_vma=False,
    )
```

profile of v0, /device:TPU:0, one launch (start us, length us, event | category | flops | bytes accessed | tf_op | source)
XLA Modules:
  0.0 1167.3 jit_solution(7776026956208568537)
XLA Ops:
  7.2 1.2 copy-done
  8.4 8.8 convert_add_fusion
  17.2 5.7 copy-done.1
  22.9 16.0 %convolution_bitcast_fusion = f32[32,1024]{1,0:T(8,128)} fusion(f32[1024,4096]{1,0:T(8,128)S(1)} %convert_add_fusion, f32[32,4096]{1,0:T(8,128)S(1)} %copy-done.3), kind=kOutput, calls=%fused_computation.3 | convolution fusion | flops 1610612736 | bytes 17432576 | tf_op jit(solution)/shard_map/dot_general | solution.py:39
  39.1 127.2 %all-reduce.10.cloned.1.call-done = f32[32,1024]{1,0:T(8,128)} async-done(((f32[32,1024]{1,0:T(8,128)}), f32[32,1024]{1,0:T(8,128)}) %all-reduce.10.cloned.1.call-update) | async-done | bytes 131088 | tf_op jit(solution)/shard_map/psum | solution.py:46
  167.4 1.2 fusion.236
  202.1 1.3 fusion.235
  251.6 13.9 %fusion.267 = f32[32,4096]{1,0:T(8,128)} fusion(f32[32,1024]{1,0:T(8,128)S(1)} %scatter.371, f32[1024,4096]{1,0:T(8,128)} %copy-done.1), kind=kOutput, calls=%fused_computation.560 | convolution fusion | flops 1610612736 | bytes 17432576 | tf_op jit(solution)/shard_map/dot_general | solution.py:48
  265.6 128.2 %all-reduce.12.cloned.1.call-done = f32[32,4096]{1,0:T(8,128)} async-done(((f32[32,4096]{1,0:T(8,128)}), f32[32,4096]{1,0:T(8,128)}) %all-reduce.12.cloned.1.call-update) | async-done | bytes 524304 | tf_op jit(solution)/shard_map/psum | solution.py:52
  393.8 19.3 %fusion.3 = f32[32,1024]{1,0:T(8,128)} fusion(f32[1024,4096]{1,0:T(8,128)} %copy-done.1, f32[32,4096]{1,0:T(8,128)} %all-reduce.12.cloned.1.call-done), kind=kOutput, calls=%fused_computation.103 | convolution fusion | flops 1610743808 | bytes 17432576 | tf_op jit(solution)/shard_map/dot_general | solution.py:39
  413.2 123.6 %all-reduce.14.cloned.1.call-done = f32[32,1024]{1,0:T(8,128)} async-done(((f32[32,1024]{1,0:T(8,128)}), f32[32,1024]{1,0:T(8,128)}) %all-reduce.14.cloned.1.call-update) | async-done | bytes 131088 | tf_op jit(solution)/shard_map/psum | solution.py:46
  537.9 1.2 fusion.234
  573.0 1.3 fusion.233
  622.4 13.9 %fusion.298 = f32[32,4096]{1,0:T(8,128)} fusion(f32[32,1024]{1,0:T(8,128)S(1)} %scatter.425, f32[1024,4096]{1,0:T(8,128)} %copy-done.1), kind=kOutput, calls=%fused_computation.591 | convolution fusion | flops 1610612736 | bytes 17432576 | tf_op jit(solution)/shard_map/dot_general | solution.py:48
  636.5 128.1 %all-reduce.16.cloned.1.call-done = f32[32,4096]{1,0:T(8,128)} async-done(((f32[32,4096]{1,0:T(8,128)}), f32[32,4096]{1,0:T(8,128)}) %all-reduce.16.cloned.1.call-update) | async-done | bytes 524304 | tf_op jit(solution)/shard_map/psum | solution.py:52
  764.6 19.3 %fusion.1 = f32[32,1024]{1,0:T(8,128)} fusion(f32[1024,4096]{1,0:T(8,128)} %copy-done.1, f32[32,4096]{1,0:T(8,128)} %all-reduce.16.cloned.1.call-done), kind=kOutput, calls=%fused_computation.101 | convolution fusion | flops 1610743808 | bytes 17432576 | tf_op jit(solution)/shard_map/dot_general | solution.py:39
  784.0 123.6 %all-reduce.18.cloned.1.call-done = f32[32,1024]{1,0:T(8,128)} async-done(((f32[32,1024]{1,0:T(8,128)}), f32[32,1024]{1,0:T(8,128)}) %all-reduce.18.cloned.1.call-update) | async-done | bytes 131088 | tf_op jit(solution)/shard_map/psum | solution.py:46
  908.6 1.2 fusion.232
  943.3 1.3 fusion.231
  992.7 14.1 %fusion.329 = f32[32,4096]{1,0:T(8,128)} fusion(f32[32,1024]{1,0:T(8,128)S(1)} %scatter.479, f32[1024,4096]{1,0:T(8,128)} %copy-done.1), kind=kOutput, calls=%fused_computation.622 | convolution fusion | flops 1610612736 | bytes 17432576 | tf_op jit(solution)/shard_map/dot_general | solution.py:48
  1006.8 128.3 %all-reduce.20.cloned.1.call-done = f32[32,4096]{1,0:T(8,128)} async-done(((f32[32,4096]{1,0:T(8,128)}), f32[32,4096]{1,0:T(8,128)}) %all-reduce.20.cloned.1.call-update) | async-done | bytes 524304 | tf_op jit(solution)/shard_map/psum | solution.py:54
  1135.0 1.1 broadcast_multiply_fusion
  1136.1 13.6 %fusion.330 = f32[1024,4096]{1,0:T(8,128)S(1)} fusion(f32[32,1024]{1,0:T(8,128)S(1)} %scatter.479, f32[32,4096]{1,0:T(8,128)S(1)} %broadcast_multiply_fusion), kind=kOutput, calls=%fused_computation.623 | convolution fusion | flops 1610612736 | bytes 17432576 | tf_op jit(solution)/shard_map/dot_general | solution.py:20
  1149.7 9.6 fusion
  (501 shorter events, 181.3 us)
Async XLA Ops:
  7.2 1.2 copy-start
  7.2 15.7 %copy-start.3 = (f32[32,4096]{1,0:T(8,128)S(1)}, f32[32,4096]{1,0:T(8,128)}, u32[]{:S(2)}) copy-start(f32[32,4096]{1,0:T(8,128)} %param.200) | copy-start | bytes 1572868
  7.2 159.1 %all-reduce.10.cloned.1.call-start = ((), (), s32[]{:S(2)}) async-start(), calls=%async_computation | async-start | bytes 262144 | tf_op jit(solution)/shard_map/psum | solution.py:46
  17.2 5.7 copy-start.1
  38.9 354.9 %all-reduce.12.cloned.1.call-start = ((), (), s32[]{:S(2)}) async-start(), calls=%async_computation.1 | async-start | bytes 1048576 | tf_op jit(solution)/shard_map/psum | solution.py:52
  265.5 271.2 %all-reduce.14.cloned.1.call-start = ((), (), s32[]{:S(2)}) async-start(), calls=%async_computation.2 | async-start | bytes 262144 | tf_op jit(solution)/shard_map/psum | solution.py:46
  413.1 351.5 %all-reduce.16.cloned.1.call-start = ((), (), s32[]{:S(2)}) async-start(), calls=%async_computation.3 | async-start | bytes 1048576 | tf_op jit(solution)/shard_map/psum | solution.py:52
  636.3 271.2 %all-reduce.18.cloned.1.call-start = ((), (), s32[]{:S(2)}) async-start(), calls=%async_computation.4 | async-start | bytes 262144 | tf_op jit(solution)/shard_map/psum | solution.py:46
  783.9 351.1 %all-reduce.20.cloned.1.call-start = ((), (), s32[]{:S(2)}) async-start(), calls=%async_computation.5 | async-start | bytes 1048576 | tf_op jit(solution)/shard_map/psum | solution.py:54
  1136.1 23.2 %copy-start.2 = (f32[32,4096]{1,0:T(8,128)}, f32[32,4096]{1,0:T(8,128)S(1)}, u32[]{:S(2)}) copy-start(f32[32,4096]{1,0:T(8,128)S(1)} %broadcast_multiply_fusion) | copy-start | bytes 1572868
  1149.7 9.6 copy-start.4
Sparse Core Ops, SparseCore 0:
  39.0 127.2 all-reduce.9
  265.7 128.1 all-reduce.11
  413.3 123.4 all-reduce.13
  636.4 128.1 all-reduce.15
  784.0 123.4 all-reduce.17
  1006.9 128.0 all-reduce.19
where the time goes:
time: 1180 us; the launch traced here: 1170 us
  waiting for transfers between devices  759 us (64%)
  matrix products  229 us (19%)
  between operations  83.2 us (7%)
  other arithmetic  69.8 us (6%)
  local copies, waits for them, and re-layouts  25.2 us (2%)
    psum x3, waiting for transfers between devices, shards(): factor = lax.psum(local_q, 'rep') / count  385 us
    psum x3, waiting for transfers between devices, shards(): total_p = lax.psum(local_p, 'rep')  374 us
    dot_general x96, matrix products, orthonormal(): coef = jnp.dot(basis, vector, precision=lax.Precision.HIGHEST)  89.7 us
    reduce_sum x96, other arithmetic, orthonormal(): basis = basis.at[k].set(vector / jnp.sqrt(jnp.sum(vector * vector) + 1.0))  57.8 us
    dot_general x3, matrix products, shards(): lax.dot_general(factor, merged, (((1,), (1,)), ((), ())), precision=lax.P...  54.5 us
    dot_general x3, matrix products, shards(): jnp.dot(basis, merged, precision=lax.Precision.HIGHEST, preferred_element...  41.9 us
  transfers between devices with their start and end apart: 6, of which 6 were waited for; matrix products, arithmetic and copies ran while one was open for 0% of the time, Pallas kernels for 0%

commit v1 on v0

--- a/solution.py
+++ b/solution.py
@@ -43,7 +43,7 @@
             precision=lax.Precision.HIGHEST,
             preferred_element_type=jnp.float32,
         )
-        total_p = lax.psum(local_p, "rep")
+        total_p = jnp.sum(lax.all_gather(local_p, "rep"), axis=0)
         basis = orthonormal(total_p)
         local_q = jnp.dot(
             basis, merged, precision=lax.Precision.HIGHEST, preferred_element_type=jnp.float32

time: 1180 us -> 984 us (0.83)
  waiting for transfers between devices: 759 us -> 570 us
    psum x3 -> x0, waiting for transfers between devices: 374 us -> none  [shards(): total_p = lax.psum(local_p, 'rep')]
    all_gather x0 -> x3, waiting for transfers between devices: none -> 186 us  [shards(): total_p = jnp.sum(lax.all_gather(local_p, 'rep'), axis=0)]
where the time goes in v1:
time: 984 us; the launch traced here: 974 us
  waiting for transfers between devices  570 us (58%)
  matrix products  225 us (23%)
  between operations  83.3 us (8%)
  other arithmetic  77.1 us (8%)
  local copies, waits for them, and re-layouts  18.2 us (2%)
    psum x3, waiting for transfers between devices, shards(): factor = lax.psum(local_q, 'rep') / count  384 us
    all_gather x3, waiting for transfers between devices, shards(): total_p = jnp.sum(lax.all_gather(local_p, 'rep'), axis=0)  186 us
    dot_general x96, matrix products, orthonormal(): coef = jnp.dot(basis, vector, precision=lax.Precision.HIGHEST)  85.3 us
    reduce_sum x96, other arithmetic, orthonormal(): basis = basis.at[k].set(vector / jnp.sqrt(jnp.sum(vector * vector) + 1.0))  57.8 us
    dot_general x3, matrix products, shards(): lax.dot_general(factor, merged, (((1,), (1,)), ((), ())), precision=lax.P...  54.5 us
    dot_general x3, matrix products, shards(): jnp.dot(basis, merged, precision=lax.Precision.HIGHEST, preferred_element...  41.7 us
    dot_general x96, matrix products, orthonormal(): vector = vector - jnp.dot(coef, basis, precision=lax.Precision.HIGHEST)  20.9 us
  transfers between devices with their start and end apart: 6, of which 6 were waited for; matrix products, arithmetic and copies ran while one was open for 0% of the time, Pallas kernels for 0%

profile of v1, /device:TPU:0, one launch (start us, length us, event | category | flops | bytes accessed | tf_op | source)
XLA Modules:
  0.0 974.0 jit_solution(2108467096827677061)
XLA Ops:
  7.2 1.2 copy-done
  8.4 8.8 convert_add_fusion
  17.2 5.7 copy-done.2
  22.9 16.0 %convolution_bitcast_fusion = f32[32,1024]{1,0:T(8,128)} fusion(f32[1024,4096]{1,0:T(8,128)S(1)} %convert_add_fusion, f32[32,4096]{1,0:T(8,128)S(1)} %copy-done.7), kind=kOutput, calls=%fused_computation.3 | convolution fusion | flops 1610612736 | bytes 17432576 | tf_op jit(solution)/shard_map/dot_general | solution.py:39
  39.1 64.4 %all-gather.7.cloned.1.call-done = f32[1024,1024]{1,0:T(8,128)} async-done(((f32[32,1024]{1,0:T(8,128)}), f32[1024,1024]{1,0:T(8,128)}) %all-gather.7.cloned.1.call-update) | async-done | bytes 4194320 | tf_op jit(solution)/shard_map/all_gather | solution.py:46
  103.5 2.4 reduce_sum.891
  127.6 0.9 convolution_bitcast_fusion.87
  187.4 13.9 %fusion.267 = f32[32,4096]{1,0:T(8,128)} fusion(f32[32,1024]{1,0:T(8,128)S(1)} %scatter.371, f32[1024,4096]{1,0:T(8,128)} %copy-done.2), kind=kOutput, calls=%fused_computation.560 | convolution fusion | flops 1610612736 | bytes 17432576 | tf_op jit(solution)/shard_map/dot_general | solution.py:48
  201.4 128.0 %all-reduce.7.cloned.1.call-done = f32[32,4096]{1,0:T(8,128)} async-done(((f32[32,4096]{1,0:T(8,128)}), f32[32,4096]{1,0:T(8,128)}) %all-reduce.7.cloned.1.call-update) | async-done | bytes 524304 | tf_op jit(solution)/shard_map/psum | solution.py:52
  329.4 19.3 %fusion.3 = f32[32,1024]{1,0:T(8,128)} fusion(f32[1024,4096]{1,0:T(8,128)} %copy-done.2, f32[32,4096]{1,0:T(8,128)} %all-reduce.7.cloned.1.call-done), kind=kOutput, calls=%fused_computation.103 | convolution fusion | flops 1610743808 | bytes 17432576 | tf_op jit(solution)/shard_map/dot_general | solution.py:39
  348.7 60.9 %all-gather.9.cloned.1.call-done = f32[1024,1024]{1,0:T(8,128)} async-done(((f32[32,1024]{1,0:T(8,128)}), f32[1024,1024]{1,0:T(8,128)}) %all-gather.9.cloned.1.call-update) | async-done | bytes 4194320 | tf_op jit(solution)/shard_map/all_gather | solution.py:46
  409.6 2.4 reduce_sum.924
  488.5 0.9 convolution_bitcast_fusion.34
  493.7 13.9 %fusion.298 = f32[32,4096]{1,0:T(8,128)} fusion(f32[32,1024]{1,0:T(8,128)S(1)} %scatter.425, f32[1024,4096]{1,0:T(8,128)} %copy-done.2), kind=kOutput, calls=%fused_computation.591 | convolution fusion | flops 1610612736 | bytes 17432576 | tf_op jit(solution)/shard_map/dot_general | solution.py:48
  507.9 127.8 %all-reduce.9.cloned.1.call-done = f32[32,4096]{1,0:T(8,128)} async-done(((f32[32,4096]{1,0:T(8,128)}), f32[32,4096]{1,0:T(8,128)}) %all-reduce.9.cloned.1.call-update) | async-done | bytes 524304 | tf_op jit(solution)/shard_map/psum | solution.py:52
  635.6 19.3 %fusion.1 = f32[32,1024]{1,0:T(8,128)} fusion(f32[1024,4096]{1,0:T(8,128)} %copy-done.2, f32[32,4096]{1,0:T(8,128)} %all-reduce.9.cloned.1.call-done), kind=kOutput, calls=%fused_computation.101 | convolution fusion | flops 1610743808 | bytes 17432576 | tf_op jit(solution)/shard_map/dot_general | solution.py:39
  655.0 60.9 %all-gather.11.cloned.1.call-done = f32[1024,1024]{1,0:T(8,128)} async-done(((f32[32,1024]{1,0:T(8,128)}), f32[1024,1024]{1,0:T(8,128)}) %all-gather.11.cloned.1.call-update) | async-done | bytes 4194320 | tf_op jit(solution)/shard_map/all_gather | solution.py:46
  715.9 2.4 reduce_sum.957
  786.9 0.9 convolution_bitcast_fusion.5
  799.8 13.9 %fusion.329 = f32[32,4096]{1,0:T(8,128)} fusion(f32[32,1024]{1,0:T(8,128)S(1)} %scatter.479, f32[1024,4096]{1,0:T(8,128)} %copy-done.2), kind=kOutput, calls=%fused_computation.622 | convolution fusion | flops 1610612736 | bytes 17432576 | tf_op jit(solution)/shard_map/dot_general | solution.py:48
  813.7 128.0 %all-reduce.11.cloned.1.call-done = f32[32,4096]{1,0:T(8,128)} async-done(((f32[32,4096]{1,0:T(8,128)}), f32[32,4096]{1,0:T(8,128)}) %all-reduce.11.cloned.1.call-update) | async-done | bytes 524304 | tf_op jit(solution)/shard_map/psum | solution.py:54
  941.8 1.1 broadcast_multiply_fusion
  942.9 13.6 %fusion.330 = f32[1024,4096]{1,0:T(8,128)S(1)} fusion(f32[32,1024]{1,0:T(8,128)S(1)} %scatter.479, f32[32,4096]{1,0:T(8,128)S(1)} %broadcast_multiply_fusion), kind=kOutput, calls=%fused_computation.623 | convolution fusion | flops 1610612736 | bytes 17432576 | tf_op jit(solution)/shard_map/dot_general | solution.py:20
  956.5 9.6 fusion
  (512 shorter events, 174.6 us)
Async XLA Ops:
  7.2 1.2 copy-start
  7.2 15.7 %copy-start.7 = (f32[32,4096]{1,0:T(8,128)S(1)}, f32[32,4096]{1,0:T(8,128)}, u32[]{:S(2)}) copy-start(f32[32,4096]{1,0:T(8,128)} %param.200) | copy-start | bytes 1572868
  7.2 96.3 %all-gather.7.cloned.1.call-start = ((), (), s32[]{:S(2)}) async-start(), calls=%async_computation.3 | async-start | bytes 4325376 | tf_op jit(solution)/shard_map/all_gather | solution.py:46
  17.2 5.7 copy-start.2
  38.9 290.5 %all-reduce.7.cloned.1.call-start = ((), (), s32[]{:S(2)}) async-start(), calls=%async_computation | async-start | bytes 1048576 | tf_op jit(solution)/shard_map/psum | solution.py:52
  105.9 3.6 copy-start.4
  201.4 208.2 %all-gather.9.cloned.1.call-start = ((), (), s32[]{:S(2)}) async-start(), calls=%async_computation.4 | async-start | bytes 4325376 | tf_op jit(solution)/shard_map/all_gather | solution.py:46
  348.7 287.0 %all-reduce.9.cloned.1.call-start = ((), (), s32[]{:S(2)}) async-start(), calls=%async_computation.1 | async-start | bytes 1048576 | tf_op jit(solution)/shard_map/psum | solution.py:52
  412.0 3.6 copy-start.5
  507.6 208.2 %all-gather.11.cloned.1.call-start = ((), (), s32[]{:S(2)}) async-start(), calls=%async_computation.5 | async-start | bytes 4325376 | tf_op jit(solution)/shard_map/all_gather | solution.py:46
  655.0 286.8 %all-reduce.11.cloned.1.call-start = ((), (), s32[]{:S(2)}) async-start(), calls=%async_computation.2 | async-start | bytes 1048576 | tf_op jit(solution)/shard_map/psum | solution.py:54
  718.3 3.6 copy-start.3
  942.8 23.2 %copy-start.6 = (f32[32,4096]{1,0:T(8,128)}, f32[32,4096]{1,0:T(8,128)S(1)}, u32[]{:S(2)}) copy-start(f32[32,4096]{1,0:T(8,128)S(1)} %broadcast_multiply_fusion) | copy-start | bytes 1572868
  942.8 24.1 %copy-start.1 = (bf16[512,1024]{1,0:T(8,128)(2,1)S(1)}, bf16[512,1024]{1,0:T(8,128)(2,1)}, u32[]{:S(2)}) copy-start(bf16[512,1024]{1,0:T(8,128)(2,1)} %param.197) | copy-start | bytes 3145732
  956.5 9.6 copy-start.8
Sparse Core Ops, SparseCore 0:
  39.0 64.4 all-gather.6
  201.5 127.8 all-reduce.6
  348.8 60.7 all-gather.8
  507.8 127.8 all-reduce.8
  655.1 60.7 all-gather.10
  813.9 127.8 all-reduce.10
